TPU v7x, 32 devices: a whole 2x2x4 slice. The times are simulated.
32 devices in a mesh: row: 4 (over z), col: 8 (over y, x, core).
Axes of the slice: x: 2, y: 2, z: 4, core: 2. Of those that a mesh axis runs over, the one named last changes fastest.
Arguments:
- right_side: float32 [16, 1024, 3072], P(None, 'row', 'col'), may hold values from -100 to 100
- cond_x: float32 [1024, 3072], P('row', 'col'), may hold values from 0.25 to 4
- cond_y: float32 [1024, 3072], P('row', 'col'), may hold values from 0.25 to 4
- pad_mask: int32 [1024, 3072], P('row', 'col'), may hold values 0 or 1
Outputs:
- solution: float32 [16, 1024, 3072], P(None, 'row', 'col')
- residual: float32 [16, 1024, 3072], P(None, 'row', 'col')
All inputs are finite; a program needn't handle non-finite values. No bound on the sum of `pad_mask` on one device may be relied on, other than what follows from the above.
Results may differ from a plain program's by a relative error of at most 0.0003.
Values sent between devices are 32-bit elements; how exact they have to be, the bound alone decides.
A program may use at most 128 MiB of HBM per device.

v0:
```python
import jax
import jax.numpy as jnp
from jax import lax
from jax.sharding import PartitionSpec as P

ITERS = 3


exact_precision = lax.Precision.HIGHEST


def passed_along(shard, axis, by):
    peers = lax.axis_size(axis)
    pairs = [(i, i + by) for i in range(peers) if 0 <= i + by < peers]
    return lax.ppermute(shard, axis, pairs)


def extended(cells, sides, width):
    for axis, dim in sides:
        count = lax.axis_size(axis)
        ends = count - 1
        head = lax.slice_in_dim(cells, 0, width, axis=dim)
        tail = lax.slice_in_dim(cells, cells.shape[dim] - width, cells.shape[dim], axis=dim)
        cells = jnp.concatenate(
            [
                lax.ppermute(tail, axis, [(i, (i + 1) % count) for i in range(ends)]),
                cells,
                lax.ppermute(head, axis, [((i + 1) % count, i) for i in range(ends)]),
            ],
            axis=dim,
        )
    return cells


def neighbour_sum(padded, cond_x, cond_above, cond_y, cond_left):
    total = cond_x * padded[:, 2:, 1:-1] + cond_above * padded[:, :-2, 1:-1]
    return total + cond_y * padded[:, 1:-1, 2:] + cond_left * padded[:, 1:-1, :-2]


def gram(left, right):
    return jnp.einsum("kab,lab->kl", left, right, precision=exact_precision)


def combine(field, matrix):
    return jnp.einsum("kab,kl->lab", field, matrix, precision=exact_precision)


def small_solve(matrix, right):
    factor = jnp.linalg.cholesky(matrix)
    return jax.scipy.linalg.cho_solve((factor, True), right)


def shards(right_side, cond_x, cond_y, pad_mask):
    pad_nodes = pad_mask.astype(jnp.float32)
    free_nodes = 1.0 - pad_nodes
    upper_row = passed_along(cond_x[-1:], "row", 1)
    cond_above = jnp.concatenate([upper_row, cond_x[:-1]], 0)
    left_column = passed_along(cond_y[:, -1:], "col", 1)
    cond_left = jnp.concatenate([left_column, cond_y[:, :-1]], 1)
    diagonal = free_nodes * (cond_x + cond_above + cond_y + cond_left) + pad_nodes
    inverse = 1.0 / diagonal
    solution = jnp.zeros_like(right_side)
    residual = right_side
    precond = residual * inverse
    direction = precond
    gram_now = lax.psum(gram(residual, precond), ("row", "col"))
    for iteration in range(ITERS):
        padded = extended(free_nodes * direction, (("row", 1), ("col", 2)), 1)
        image = pad_nodes * direction + free_nodes * (
            diagonal * direction - neighbour_sum(padded, cond_x, cond_above, cond_y, cond_left)
        )
        weighted = image * inverse
        curvature, cross_term, image_term = lax.psum(
            (gram(direction, image), gram(image, precond), gram(image, weighted)), ("row", "col")
        )
        alpha_block = small_solve(curvature, gram_now)
        solution = solution + combine(direction, alpha_block)
        residual = residual - combine(image, alpha_block)
        precond = residual * inverse
        mixed = jnp.dot(alpha_block.T, cross_term, precision=exact_precision)
        quadratic = jnp.dot(
            jnp.dot(alpha_block.T, image_term, precision=exact_precision),
            alpha_block,
            precision=exact_precision,
        )
        gram_next = gram_now - mixed - mixed.T + quadratic
        beta_block = small_solve(gram_now, gram_next)
        direction = precond + combine(direction, beta_block)
        gram_now = gram_next
    return (solution, residual)


def solution(mesh):
    in_specs = (P(None, "row", "col"), P("row", "col"), P("row", "col"), P("row", "col"))
    out_specs = (P(None, "row", "col"), P(None, "row", "col"))
    return jax.shard_map(shards, mesh=mesh, in_specs=in_specs, out_specs=out_specs, check_vma=False)
```

profile of v0, /device:TPU:0, one launch (start us, length us, event | category | flops | bytes accessed | tf_op | source)
XLA Modules:
  0.0 509.1 jit_solution(3456726133904261827)
XLA Ops:
  1.3 4.9 collective-permute-start
  13.6 6.9 %multiply_multiply_fusion = f32[16,256,384]{2,0,1:T(8,128)S(1)} fusion(f32[16,256,384]{2,1,0:T(8,128)} %param.7, f32[256,384]{1,0:T(8,128)S(1)} %get-tuple-element.31, f32[256,384]{1,0:T(8,128)S(1)} %fusion.83), kind=kLoop, calls=%fused_computation.14 | loop fusion | flops 3145728 | bytes 13369344 | tf_op jit(solution)/shard_map/mul | solution.py:68
  42.9 30.7 %fusion.78 = f32[16,16]{0,1:T(8,128)S(1)} fusion(f32[16,256,384]{2,1,0:T(8,128)} %param.7, f32[256,384]{1,0:T(8,128)S(1)} %fusion.83), kind=kOutput, calls=%fused_computation.115 | convolution fusion | flops 303562752 | bytes 6685696 | tf_op jit(solution)/shard_map/kab,lab->kl/dot_general | solution.py:41
  78.7 21.2 %fusion.14 = f32[16,256,384]{2,0,1:T(8,128)S(1)} fusion(f32[16,258,1]{2,0,1:T(8,128)} %copy.33, f32[16,1,384]{2,0,1:T(8,128)S(1)} %collective-permute-done.2, f32[16,256,384]{2,0,1:T(8,128)} %copy-done.2, f32[16,1,384]{2,0,1:T(8,128)S(1)} %collective-permute-done.3, f32[16,258,1]{2,0,1:T(8,128)} %copy.31, f32[16,256,384]{2,1,0:T(8,128)} %param.7, ...), kind=kLoop, calls=%fused_computation.17 | loop fusion | flops 33030144 | bytes 22102272 | tf_op jit(solution)/shard_map/add | solution.py:69
  99.9 8.1 %fusion.72 = f32[16,16]{1,0:T(8,128)S(1)} fusion(f32[16,256,384]{2,0,1:T(8,128)S(1)} %fusion.14, f32[256,384]{1,0:T(8,128)S(1)} %fusion.83), kind=kOutput, calls=%fused_computation.106 | convolution fusion | flops 303562752 | bytes 6685696 | tf_op jit(solution)/shard_map/kab,lab->kl/dot_general | solution.py:41
  108.1 10.6 %fusion.69 = f32[16,16]{1,0:T(8,128)S(1)} fusion(f32[16,256,384]{2,0,1:T(8,128)S(1)} %fusion.14, f32[16,256,384]{2,1,0:T(8,128)S(1)} %bitcast.144, f32[256,384]{1,0:T(8,128)S(1)} %fusion.83), kind=kOutput, calls=%fused_computation.105 | convolution fusion | flops 303562752 | bytes 12977152 | tf_op jit(solution)/shard_map/kab,lab->kl/dot_general | solution.py:41
  118.7 10.6 %fusion.66 = f32[16,16]{0,1:T(8,128)S(1)} fusion(f32[16,256,384]{2,0,1:T(8,128)S(1)} %fusion.14, f32[16,256,384]{2,1,0:T(8,128)S(1)} %bitcast.144, f32[256,384]{1,0:T(8,128)S(1)} %fusion.83), kind=kOutput, calls=%fused_computation.104 | convolution fusion | flops 303562752 | bytes 12977152 | tf_op jit(solution)/shard_map/kab,lab->kl/dot_general | solution.py:41
  129.2 45.8 %all-reduce.1 = (f32[16,16]{0,1:T(8,128)S(1)}, f32[16,16]{0,1:T(8,128)S(1)}, f32[16,16]{1,0:T(8,128)S(1)}, f32[16,16]{1,0:T(8,128)S(1)}) all-reduce(f32[16,16]{0,1:T(8,128)S(1)} %fusion.78, f32[16,16]{0,1:T(8,128)S(1)} %fusion.66, f32[16,16]{1,0:T(8,128)S(1)} %fusion.72, ...), channel_id=1, replica_groups=mesh['row'=4,'col'=8] {'row','col'}, use_global_device_ids=true, to_apply=%region_3.5 | all-reduce | flops 1024 | bytes 8192 | tf_op jit(solution)/shard_map/psum | solution.py:66
  183.6 13.2 %copy_subtract_fusion = f32[16,256,384]{2,0,1:T(8,128)} fusion(f32[16,256,384]{2,1,0:T(8,128)} %param.7, f32[16,256,384]{2,0,1:T(8,128)} %copy-done, f32[16,16]{1,0:T(8,128)S(1)} %fusion.111), kind=kOutput, calls=%fused_computation.80 | convolution fusion | flops 303562752 | bytes 18875392 | tf_op jit(solution)/shard_map/kab,kl->lab/dot_general | solution.py:45
  199.5 15.0 %broadcast_multiply_fusion.1 = (f32[16,256,384]{2,0,1:T(8,128)S(1)}, f32[16,256,384]{2,0,1:T(8,128)}) fusion(f32[256,384]{1,0:T(8,128)S(1)} %get-tuple-element.31, f32[16,16,1]{0,1,2:T(8,128)S(1)} %convolution_bitcast_fusion.4, f32[16,256,384]{2,1,0:T(8,128)} %param.7, f32[256,384]{1,0:T(8,128)S(1)} %fusion.83, f32[16,256,384]{2,0,1:T(8,128)} %copy_subtract_fusion), kind=kOutput, calls=%fused_computation.83 | convolution fusion | flops 308281344 | bytes 25953280 | tf_op jit(solution)/shard_map/kab,kl->lab/dot_general | solution.py:45
  242.5 20.3 %fusion.31 = f32[16,256,384]{2,0,1:T(8,128)S(1)} fusion(f32[16,258,1]{2,0,1:T(8,128)} %copy.46, f32[16,1,384]{2,0,1:T(8,128)S(1)} %collective-permute-done.6, f32[16,256,384]{2,0,1:T(8,128)} %copy-done.4, f32[16,1,384]{2,0,1:T(8,128)S(1)} %collective-permute-done.7, f32[16,258,1]{2,0,1:T(8,128)} %copy.44, f32[16,256,384]{2,0,1:T(8,128)} %get-tuple-element.33, ...), kind=kLoop, calls=%fused_computation.43 | loop fusion | flops 31457280 | bytes 21709056 | tf_op jit(solution)/shard_map/add | solution.py:69
  262.9 8.1 %fusion.75 = f32[16,16]{1,0:T(8,128)S(1)} fusion(f32[16,256,384]{2,0,1:T(8,128)S(1)} %fusion.31, f32[256,384]{1,0:T(8,128)S(1)} %fusion.83), kind=kOutput, calls=%fused_computation.107 | convolution fusion | flops 303562752 | bytes 6685696 | tf_op jit(solution)/shard_map/kab,lab->kl/dot_general | solution.py:41
  271.1 8.3 %fusion.63 = f32[16,16]{1,0:T(8,128)S(1)} fusion(f32[16,256,384]{2,0,1:T(8,128)S(1)} %fusion.31, f32[16,256,384]{2,0,1:T(8,128)S(1)} %bitcast.150, f32[256,384]{1,0:T(8,128)S(1)} %fusion.83), kind=kOutput, calls=%fused_computation.103 | convolution fusion | flops 303562752 | bytes 12977152 | tf_op jit(solution)/shard_map/kab,lab->kl/dot_general | solution.py:41
  279.5 8.5 %convolution_bitcast_fusion.3 = f32[16,16]{0,1:T(8,128)S(1)} fusion(f32[16,256,384]{2,0,1:T(8,128)S(1)} %bitcast.148, f32[16,256,384]{2,0,1:T(8,128)S(1)} %fusion.31), kind=kOutput, calls=%fused_computation.112 | convolution fusion | flops 301989888 | bytes 12583936 | tf_op jit(solution)/shard_map/kab,lab->kl/dot_general | solution.py:41
  287.9 41.7 %all-reduce = (f32[16,16]{0,1:T(8,128)S(1)}, f32[16,16]{1,0:T(8,128)S(1)}, f32[16,16]{1,0:T(8,128)S(1)}) all-reduce(f32[16,16]{0,1:T(8,128)S(1)} %convolution_bitcast_fusion.3, f32[16,16]{1,0:T(8,128)S(1)} %fusion.75, f32[16,16]{1,0:T(8,128)S(1)} %fusion.63), channel_id=1, replica_groups=mesh['row'=4,'col'=8] {'row','col'}, use_global_device_ids=true, to_apply=%region_6.0 | all-reduce | flops 768 | bytes 6144 | tf_op jit(solution)/shard_map/psum | solution.py:73
  334.1 10.7 %convolution_subtract_fusion.1 = f32[16,256,384]{2,0,1:T(8,128)} fusion(f32[16,256,384]{2,0,1:T(8,128)} %copy_subtract_fusion, f32[16,256,384]{2,0,1:T(8,128)} %copy-done.1, f32[16,16]{1,0:T(8,128)S(1)} %fusion.100), kind=kOutput, calls=%fused_computation.93 | convolution fusion | flops 303562752 | bytes 18875392 | tf_op jit(solution)/shard_map/kab,kl->lab/dot_general | solution.py:45
  345.9 11.0 %broadcast_multiply_fusion = (f32[16,256,384]{2,0,1:T(8,128)S(1)}, f32[16,256,384]{2,0,1:T(8,128)}) fusion(f32[256,384]{1,0:T(8,128)S(1)} %get-tuple-element.31, f32[16,16,1]{0,1,2:T(8,128)S(1)} %convolution_bitcast_fusion.2, f32[16,256,384]{2,0,1:T(8,128)} %get-tuple-element.33, f32[16,256,384]{2,0,1:T(8,128)} %convolution_subtract_fusion.1, ...), kind=kOutput, calls=%fused_computation.82 | convolution fusion | flops 306708480 | bytes 25953280 | tf_op jit(solution)/shard_map/kab,kl->lab/dot_general | solution.py:45
  376.3 9.2 %fusion.98 = f32[16,256,384]{2,0,1:T(8,128)} fusion(f32[16,256,384]{2,0,1:T(8,128)} %get-tuple-element.33, f32[16,16]{1,0:T(8,128)S(1)} %fusion.100), kind=kOutput, calls=%fused_computation.144 | convolution fusion | flops 301989888 | bytes 12583936 | tf_op jit(solution)/shard_map/kab,kl->lab/dot_general | solution.py:45
  390.6 19.7 %fusion.21 = f32[16,256,384]{2,0,1:T(8,128)S(1)} fusion(f32[16,258,1]{2,0,1:T(8,128)} %copy.57, f32[16,1,384]{2,0,1:T(8,128)S(1)} %collective-permute-done.10, f32[16,256,384]{2,0,1:T(8,128)} %copy-done.3, f32[16,1,384]{2,0,1:T(8,128)S(1)} %collective-permute-done.11, f32[16,258,1]{2,0,1:T(8,128)} %copy.55, f32[16,256,384]{2,0,1:T(8,128)} %get-tuple-element.35, ...), kind=kLoop, calls=%fused_computation.25 | loop fusion | flops 31457280 | bytes 21709056 | tf_op jit(solution)/shard_map/add | solution.py:69
  413.0 10.2 %convolution_bitcast_fusion.1 = f32[16,16]{0,1:T(8,128)S(1)} fusion(f32[16,256,384]{2,0,1:T(8,128)} %get-tuple-element.35, f32[16,256,384]{2,0,1:T(8,128)S(1)} %fusion.21), kind=kOutput, calls=%fused_computation.109 | convolution fusion | flops 301989888 | bytes 12583936 | tf_op jit(solution)/shard_map/kab,lab->kl/dot_general | solution.py:41
  423.2 43.2 %psum.63 = f32[16,16]{0,1:T(8,128)S(1)} all-reduce(f32[16,16]{0,1:T(8,128)S(1)} %convolution_bitcast_fusion.1), channel_id=1, replica_groups=mesh['row'=4,'col'=8] {'row','col'}, use_global_device_ids=true, to_apply=%region_9.12 | all-reduce | flops 256 | bytes 2048 | tf_op jit(solution)/shard_map/psum | solution.py:73
  470.9 8.9 %convolution_subtract_fusion = f32[16,256,384]{2,0,1:T(8,128)S(1)} fusion(f32[16,256,384]{2,0,1:T(8,128)} %convolution_subtract_fusion.1, f32[16,16,1]{0,1,2:T(8,128)S(1)} %convolution_bitcast_fusion, f32[16,256,384]{2,0,1:T(8,128)} %copy-done.5), kind=kOutput, calls=%fused_computation.92 | convolution fusion | flops 303562752 | bytes 18875392 | tf_op jit(solution)/shard_map/kab,kl->lab/dot_general | solution.py:45
  479.9 7.6 %fusion.123 = f32[16,256,384]{2,0,1:T(8,128)S(1)} fusion(f32[16,16,1]{0,1,2:T(8,128)S(1)} %convolution_bitcast_fusion, f32[16,256,384]{2,0,1:T(8,128)} %get-tuple-element.35), kind=kOutput, calls=%fused_computation.185 | convolution fusion | flops 301989888 | bytes 12583936 | tf_op jit(solution)/shard_map/kab,kl->lab/dot_general | solution.py:45
  487.5 12.1 %add_add_fusion = f32[16,256,384]{2,0,1:T(8,128)S(1)} fusion(f32[16,256,384]{2,0,1:T(8,128)S(1)} %fusion.123, f32[16,256,384]{2,0,1:T(8,128)} %fusion.98, f32[16,256,384]{2,1,0:T(8,128)S(1)} %bitcast.146, f32[256,384]{1,0:T(8,128)S(1)} %fusion.83, f32[16,16]{1,0:T(8,128)S(1)} %fusion.111), kind=kOutput, calls=%fused_computation.72 | convolution fusion | flops 306708480 | bytes 25560064 | tf_op jit(solution)/shard_map/kab,kl->lab/dot_general | solution.py:45
  (150 shorter events, 121.2 us)
Async XLA Ops:
  1.3 8.4 %collective-permute-start = (f32[1,384]{1,0:T(1,128)S(1)}, f32[1,384]{1,0:T(1,128)S(1)}, u32[]{:S(2)}, u32[]{:S(2)}) collective-permute-start(f32[1,384]{1,0:T(1,128)S(1)} %slice.108), channel_id=1, source_target_pairs={{0,8},{8,16},{16,24},{1,9},{9,17},{17,25},{2,10},{10,18},{18,26},{... | collective-permute-start | bytes 4616 | tf_op jit(solution)/shard_map/ppermute | solution.py:15
  7.3 2.4 collective-permute-start.1
  20.5 5.6 %collective-permute-start.3 = (f32[16,1,384]{2,0,1:T(8,128)S(1)}, f32[16,1,384]{2,0,1:T(8,128)S(1)}, u32[]{:S(2)}, u32[]{:S(2)}) collective-permute-start(f32[16,1,384]{2,0,1:T(8,128)S(1)} %get-tuple-element.29), channel_id=1, source_target_pairs={{0,8},{8,16},{16,24},{1,9},{9,17},{17,25},{2,10},{10,18},{18,26},{... | collective-permute-start | bytes 73736 | tf_op jit(solution)/shard_map/ppermute | solution.py:26
  24.0 5.7 %collective-permute-start.2 = (f32[16,1,384]{2,0,1:T(8,128)S(1)}, f32[16,1,384]{2,0,1:T(8,128)S(1)}, u32[]{:S(2)}, u32[]{:S(2)}) collective-permute-start(f32[16,1,384]{2,0,1:T(8,128)S(1)} %get-tuple-element.30), channel_id=1, source_target_pairs={{8,0},{16,8},{24,16},{9,1},{17,9},{25,17},{10,2},{18,10},{26,18},{... | collective-permute-start | bytes 73736 | tf_op jit(solution)/shard_map/ppermute | solution.py:28
  37.6 41.1 %copy-start.6 = (f32[256,384]{1,0:T(8,128)S(1)}, f32[256,384]{1,0:T(8,128)}, u32[]{:S(2)}) copy-start(f32[256,384]{1,0:T(8,128)} %param.9) | copy-start | bytes 1179652
  37.6 38.6 %collective-permute-start.5 = (f32[16,258,1]{1,0,2:T(8,128)S(1)}, f32[16,258,1]{1,0,2:T(8,128)S(1)}, u32[]{:S(2)}, u32[]{:S(2)}) collective-permute-start(f32[16,258,1]{1,0,2:T(8,128)S(1)} %copy.32), channel_id=1, source_target_pairs={{0,1},{1,2},{2,3},{3,4},{4,5},{5,6},{6,7},{8,9},{9,10},{10,11},{11... | collective-permute-start | bytes 49544 | tf_op jit(solution)/shard_map/ppermute | solution.py:26
  41.3 32.4 %collective-permute-start.4 = (f32[16,258,1]{1,0,2:T(8,128)S(1)}, f32[16,258,1]{1,0,2:T(8,128)S(1)}, u32[]{:S(2)}, u32[]{:S(2)}) collective-permute-start(f32[16,258,1]{1,0,2:T(8,128)S(1)} %copy.30), channel_id=1, source_target_pairs={{1,0},{2,1},{3,2},{4,3},{5,4},{6,5},{7,6},{9,8},{10,9},{11,10},{12... | collective-permute-start | bytes 49544 | tf_op jit(solution)/shard_map/ppermute | solution.py:28
  76.2 31.8 %slice-start = ((s8[6291456]{0:T(1024)(128)(4,1)}), s8[2097152]{0:T(1024)(128)(4,1)S(1)}, s32[]{:S(2)}) async-start(s8[6291456]{0:T(1024)(128)(4,1)} %bitcast.143), calls=%async_computation | async-start | bytes 4194304
  78.7 29.3 %slice-start.1 = ((s8[6291456]{0:T(1024)(128)(4,1)}), s8[4194304]{0:T(1024)(128)(4,1)S(1)}, s32[]{:S(2)}) async-start(s8[6291456]{0:T(1024)(128)(4,1)} %bitcast.143), calls=%async_computation.1 | async-start | bytes 8388608
  99.9 18.8 %copy-start = (f32[16,256,384]{2,0,1:T(8,128)}, f32[16,256,384]{2,0,1:T(8,128)S(1)}, u32[]{:S(2)}) copy-start(f32[16,256,384]{2,0,1:T(8,128)S(1)} %fusion.14) | copy-start | bytes 18874372
  214.5 4.3 collective-permute-start.7
  216.9 5.7 %collective-permute-start.6 = (f32[16,1,384]{2,0,1:T(8,128)S(1)}, f32[16,1,384]{2,0,1:T(8,128)S(1)}, u32[]{:S(2)}, u32[]{:S(2)}) collective-permute-start(f32[16,1,384]{2,0,1:T(8,128)S(1)} %get-tuple-element.28), channel_id=1, source_target_pairs={{8,0},{16,8},{24,16},{9,1},{17,9},{25,17},{10,2},{18,10},{26,18},{... | collective-permute-start | bytes 73736 | tf_op jit(solution)/shard_map/ppermute | solution.py:28
  230.5 9.5 %collective-permute-start.9 = (f32[16,258,1]{1,0,2:T(8,128)S(1)}, f32[16,258,1]{1,0,2:T(8,128)S(1)}, u32[]{:S(2)}, u32[]{:S(2)}) collective-permute-start(f32[16,258,1]{1,0,2:T(8,128)S(1)} %copy.45), channel_id=1, source_target_pairs={{0,1},{1,2},{2,3},{3,4},{4,5},{5,6},{6,7},{8,9},{9,10},{10,11},{11... | collective-permute-start | bytes 49544 | tf_op jit(solution)/shard_map/ppermute | solution.py:26
  231.8 5.6 %collective-permute-start.8 = (f32[16,258,1]{1,0,2:T(8,128)S(1)}, f32[16,258,1]{1,0,2:T(8,128)S(1)}, u32[]{:S(2)}, u32[]{:S(2)}) collective-permute-start(f32[16,258,1]{1,0,2:T(8,128)S(1)} %copy.43), channel_id=1, source_target_pairs={{1,0},{2,1},{3,2},{4,3},{5,4},{6,5},{7,6},{9,8},{10,9},{11,10},{12... | collective-permute-start | bytes 49544 | tf_op jit(solution)/shard_map/ppermute | solution.py:28
  240.0 31.1 %slice-start.6 = ((s8[6291456]{0:T(1024)(128)(4,1)}), s8[2097152]{0:T(1024)(128)(4,1)S(1)}, s32[]{:S(2)}) async-start(s8[6291456]{0:T(1024)(128)(4,1)} %bitcast.149), calls=%async_computation.6 | async-start | bytes 4194304
  242.5 28.5 %slice-start.7 = ((s8[6291456]{0:T(1024)(128)(4,1)}), s8[4194304]{0:T(1024)(128)(4,1)S(1)}, s32[]{:S(2)}) async-start(s8[6291456]{0:T(1024)(128)(4,1)} %bitcast.149), calls=%async_computation.7 | async-start | bytes 8388608
  356.9 4.6 collective-permute-start.11
  359.9 5.7 %collective-permute-start.10 = (f32[16,1,384]{2,0,1:T(8,128)S(1)}, f32[16,1,384]{2,0,1:T(8,128)S(1)}, u32[]{:S(2)}, u32[]{:S(2)}) collective-permute-start(f32[16,1,384]{2,0,1:T(8,128)S(1)} %get-tuple-element.26), channel_id=1, source_target_pairs={{8,0},{16,8},{24,16},{9,1},{17,9},{25,17},{10,2},{18,10},{26,18},{... | collective-permute-start | bytes 73736 | tf_op jit(solution)/shard_map/ppermute | solution.py:28
  373.6 17.0 %copy-start.7 = (f32[256,384]{1,0:T(8,128)S(1)}, f32[256,384]{1,0:T(8,128)}, u32[]{:S(2)}) copy-start(f32[256,384]{1,0:T(8,128)} %param.8) | copy-start | bytes 1179652
  373.6 17.0 %copy-start.8 = (f32[256,384]{1,0:T(8,128)S(1)}, f32[256,384]{1,0:T(8,128)}, u32[]{:S(2)}) copy-start(f32[256,384]{1,0:T(8,128)} %get-tuple-element.15) | copy-start | bytes 1179652
  373.6 17.0 %copy-start.9 = (f32[256,384]{1,0:T(8,128)S(1)}, f32[256,384]{1,0:T(8,128)}, u32[]{:S(2)}) copy-start(f32[256,384]{1,0:T(8,128)} %get-tuple-element.17) | copy-start | bytes 1179652
  373.6 14.4 %collective-permute-start.13 = (f32[16,258,1]{1,0,2:T(8,128)S(1)}, f32[16,258,1]{1,0,2:T(8,128)S(1)}, u32[]{:S(2)}, u32[]{:S(2)}) collective-permute-start(f32[16,258,1]{1,0,2:T(8,128)S(1)} %copy.56), channel_id=1, source_target_pairs={{0,1},{1,2},{2,3},{3,4},{4,5},{5,6},{6,7},{8,9},{9,10},{10,11},{11... | collective-permute-start | bytes 49544 | tf_op jit(solution)/shard_map/ppermute | solution.py:26
  375.0 10.5 %collective-permute-start.12 = (f32[16,258,1]{1,0,2:T(8,128)S(1)}, f32[16,258,1]{1,0,2:T(8,128)S(1)}, u32[]{:S(2)}, u32[]{:S(2)}) collective-permute-start(f32[16,258,1]{1,0,2:T(8,128)S(1)} %copy.54), channel_id=1, source_target_pairs={{1,0},{2,1},{3,2},{4,3},{5,4},{6,5},{7,6},{9,8},{10,9},{11,10},{12... | collective-permute-start | bytes 49544 | tf_op jit(solution)/shard_map/ppermute | solution.py:28
  413.0 74.5 %slice-start.2 = ((s8[6291456]{0:T(1024)(128)(4,1)}), s8[2097152]{0:T(1024)(128)(4,1)S(1)}, s32[]{:S(2)}) async-start(s8[6291456]{0:T(1024)(128)(4,1)} %bitcast.145), calls=%async_computation.2 | async-start | bytes 4194304
  (11 other events, 132.6 us)
where the time goes:
time: 516 us; the launch traced here: 509 us
  matrix products  186 us (36%)
  blocking collectives  131 us (25%)
  other arithmetic  101 us (20%)
  local copies, waits for them, and re-layouts  45.3 us (9%)
  starting transfers between devices  30 us (6%)
  waiting for transfers between devices  15 us (3%)
    dot_general x8, matrix products, gram(): return jnp.einsum('kab,lab->kl', left, right, precision=exact_precision)  95.2 us
    dot_general x8, matrix products, combine(): return jnp.einsum('kab,kl->lab', field, matrix, precision=exact_precision)  87.7 us
    psum x2, blocking collectives, shards(): lax.psum((gram(direction, image), gram(image, precond), gram(image, weigh...  84.9 us
    add x3, other arithmetic, shards(): pad_nodes * direction  61.2 us
    psum x1, blocking collectives, shards(): gram_now = lax.psum(gram(residual, precond), ('row', 'col'))  45.8 us
    ppermute x6, starting transfers between devices, extended(): lax.ppermute(tail, axis, [(i, (i + 1) % count) for i in range(ends)])  15.2 us
    ppermute x6, waiting for transfers between devices, extended(): lax.ppermute(head, axis, [((i + 1) % count, i) for i in range(ends)])  14 us
    unnamed x44, local copies, waits for them, and re-layouts  12.1 us
  transfers between devices with their start and end apart: 14, of which 5 were waited for; matrix products, arithmetic and copies ran while one was open for 10% of the time, Pallas kernels for 0%

commit v1 on v0

v1 whole, which is shorter than its diff:
```python
import functools

import jax
import jax.numpy as jnp
from jax import lax
from jax.experimental import pallas as pl
from jax.experimental.pallas import tpu as pltpu
from jax.sharding import PartitionSpec as P

ITERS = 3
F32 = jnp.float32
BF16 = jnp.bfloat16
MESH = pl.DeviceIdType.MESH
SUB = 8
LANES = 128


def exact_dot(left, right, dims):
    return lax.dot_general(
        left, right, (dims, ((), ())), precision=lax.Precision.HIGHEST, preferred_element_type=F32
    )


def fast_dot(left, right, dims):
    return lax.dot_general(left, right, (dims, ((), ())), preferred_element_type=F32)


def split(value):
    high = value.astype(BF16)
    low = (value - high.astype(F32)).astype(BF16)
    return high, low


def iota(shape, dim):
    return lax.broadcasted_iota(jnp.int32, shape, dim)


def kernel(
    nr, nc, b_ref, cx_ref, cy_ref, pad_ref, sol_ref, res_ref,
    v_ref, img_ref, ex_ref, ea_ref, ey_ref, el_ref, dg_ref, inv_ref,
    gram_ref, g0_ref,
    crow_src, crow_dst, ccol_src, ccol_dst,
    vrow_src, vrow_dst, vcol_src, vcol_dst,
    row_slots, col_slots, row_mine, col_mine,
    halo_send, halo_recv, red_send, red_recv,
):
    fields, rows, cols = b_ref.shape
    wide = fields * SUB
    tiles = rows // SUB
    pairs = tiles // 2
    row = lax.axis_index("row")
    col = lax.axis_index("col")

    barrier = pltpu.get_barrier_semaphore()
    for d in range(1, nr):
        pl.semaphore_signal(barrier, inc=1, device_id=(lax.rem(row + d, nr), col), device_id_type=MESH)
    for d in range(1, nc):
        pl.semaphore_signal(barrier, inc=1, device_id=(row, lax.rem(col + d, nc)), device_id_type=MESH)
    pl.semaphore_wait(barrier, nr - 1 + nc - 1)

    has_out = (row < nr - 1, row > 0, col < nc - 1, col > 0)
    has_in = (row > 0, row < nr - 1, col > 0, col < nc - 1)
    targets = ((row + 1, col), (row - 1, col), (row, col + 1), (row, col - 1))

    def halo_copy(stage, side, row_src, row_dst, col_src, col_dst):
        src, dst = (row_src, row_dst) if side < 2 else (col_src, col_dst)
        return pltpu.make_async_remote_copy(
            src_ref=src.at[side % 2],
            dst_ref=dst.at[side % 2],
            send_sem=halo_send.at[stage, side],
            recv_sem=halo_recv.at[stage, side],
            device_id=targets[side],
            device_id_type=MESH,
        )

    def halo_start(stage, *bufs):
        for side in range(4):
            @pl.when(has_out[side])
            def _():
                halo_copy(stage, side, *bufs).start()

    def halo_wait(stage, *bufs):
        for side in range(4):
            @pl.when(has_out[side])
            def _():
                halo_copy(stage, side, *bufs).wait_send()

            @pl.when(has_in[side])
            def _():
                halo_copy(stage, side, *bufs).wait_recv()

            dst = bufs[1] if side < 2 else bufs[3]

            @pl.when(jnp.logical_not(has_in[side]))
            def _():
                dst[side % 2] = jnp.zeros(dst.shape[1:], F32)

    lane8 = iota((SUB, LANES), 1)
    pad = pad_ref[...].astype(F32)
    free = 1.0 - pad
    cx = cx_ref[...]
    cy = cy_ref[...]

    def packed_column(array, lane):
        base = lane // LANES * LANES
        out = jnp.zeros((SUB, LANES), F32)
        for r in range(tiles):
            tile = array[r * SUB:(r + 1) * SUB, base:base + LANES]
            out = jnp.where(lane8 == r, pltpu.roll(tile, (r - lane) % LANES, 1), out)
        return out

    def unpacked_column(packed, lane):
        return jnp.concatenate(
            [pltpu.roll(packed, (lane - r) % LANES, 1) for r in range(tiles)], axis=0
        )

    crow_src[0, 0:1, :] = cx[rows - 1:rows]
    crow_src[0, 1:2, :] = free[rows - 1:rows]
    crow_src[0, 2:SUB, :] = jnp.zeros((SUB - 2, cols), F32)
    crow_src[1] = jnp.broadcast_to(free[0:1], (SUB, cols))
    ccol_src[0, 0:SUB] = packed_column(cy, cols - 1)
    ccol_src[0, SUB:] = packed_column(free, cols - 1)
    first = packed_column(free, 0)
    ccol_src[1, 0:SUB] = first
    ccol_src[1, SUB:] = first
    cond_bufs = (crow_src, crow_dst, ccol_src, ccol_dst)
    halo_start(0, *cond_bufs)
    halo_wait(0, *cond_bufs)

    rowi = iota((rows, cols), 0)
    lane = iota((rows, LANES), 1)

    def from_above(array, halo):
        return jnp.where(rowi == 0, halo, pltpu.roll(array, 1, 0))

    def from_below(array, halo):
        return jnp.where(rowi == rows - 1, halo, pltpu.roll(array, rows - 1, 0))

    def from_left(array, halo):
        rolled = pltpu.roll(array, 1, 1)
        edge = jnp.where(lane == 0, halo, rolled[:, :LANES])
        return edge if cols == LANES else jnp.concatenate([edge, rolled[:, LANES:]], axis=1)

    def from_right(array, halo):
        rolled = pltpu.roll(array, cols - 1, 1)
        edge = jnp.where(lane == LANES - 1, halo, rolled[:, cols - LANES:])
        return edge if cols == LANES else jnp.concatenate([rolled[:, :cols - LANES], edge], axis=1)

    cx_up = crow_dst[0, 0:1, :]
    cond_above = from_above(cx, cx_up)
    cond_left = from_left(cy, unpacked_column(ccol_dst[0, 0:SUB], 0))
    diagonal = free * (cx + cond_above + cy + cond_left) + pad
    dg_ref[...] = diagonal
    inv_ref[...] = 1.0 / diagonal
    ex_ref[...] = free * cx * from_below(free, crow_dst[1, 0:1, :])
    ea_ref[...] = free * cond_above * from_above(free, crow_dst[0, 1:2, :])
    ey_ref[...] = free * cy * from_right(free, unpacked_column(ccol_dst[1, 0:SUB], LANES - 1))
    el_ref[...] = free * cond_left * from_left(free, unpacked_column(ccol_dst[0, SUB:], 0))

    lane_w = iota((wide, LANES), 1)
    lane3 = iota((fields, SUB, LANES), 2)
    sub3 = iota((fields, SUB, cols), 1)

    def rows_at(r):
        return pl.ds(pl.multiple_of(r * SUB, SUB), SUB)

    def store_direction(stage, r, value):
        v_ref[:, rows_at(r + 1), :] = value.reshape(fields, SUB, cols)
        right = pltpu.roll(value[:, cols - LANES:], lax.rem(r + 1, LANES), 1)
        left = pltpu.roll(value[:, :LANES], lax.rem(r + LANES, LANES), 1)
        hit = lane_w == r
        vcol_src[stage, 0] = jnp.where(hit, right, vcol_src[stage, 0])
        vcol_src[stage, 1] = jnp.where(hit, left, vcol_src[stage, 1])

    def direction_bufs(stage):
        return (vrow_src.at[stage], vrow_dst.at[stage], vcol_src.at[stage], vcol_dst.at[stage])

    def direction_start(stage):
        vrow_src[stage, 0] = v_ref[:, rows:rows + SUB, :][:, SUB - 1, :]
        vrow_src[stage, 1] = v_ref[:, SUB:2 * SUB, :][:, 0, :]
        halo_start(stage + 1, *direction_bufs(stage))

    def direction_wait(stage):
        halo_wait(stage + 1, *direction_bufs(stage))
        top = vrow_dst[stage, 0]
        bottom = vrow_dst[stage, 1]
        v_ref[:, 0:SUB, :] = jnp.broadcast_to(top[:, None, :], (fields, SUB, cols))
        v_ref[:, rows + SUB:, :] = jnp.broadcast_to(bottom[:, None, :], (fields, SUB, cols))

    def operate(stage, r):
        cur = v_ref[:, rows_at(r + 1), :]
        prev = v_ref[:, rows_at(r), :]
        after = v_ref[:, rows_at(r + 2), :]
        up = pltpu.roll(jnp.where(sub3 == SUB - 1, prev, cur), 1, 1)
        down = pltpu.roll(jnp.where(sub3 == 0, after, cur), SUB - 1, 1)
        left = pltpu.roll(cur, 1, 2)
        right = pltpu.roll(cur, cols - 1, 2)
        halo_left = pltpu.roll(vcol_dst[stage, 0], lax.rem(LANES - r, LANES), 1)
        halo_right = pltpu.roll(vcol_dst[stage, 1], LANES - 1 - r, 1)
        edge_left = jnp.where(lane3 == 0, halo_left.reshape(fields, SUB, LANES), left[:, :, :LANES])
        edge_right = jnp.where(
            lane3 == LANES - 1, halo_right.reshape(fields, SUB, LANES), right[:, :, cols - LANES:]
        )
        if cols > LANES:
            edge_left = jnp.concatenate([edge_left, left[:, :, LANES:]], axis=2)
            edge_right = jnp.concatenate([right[:, :, :cols - LANES], edge_right], axis=2)
        at = rows_at(r)
        image = (
            dg_ref[at, :][None] * cur
            - (ex_ref[at, :][None] * down + ea_ref[at, :][None] * up)
            - (ey_ref[at, :][None] * edge_right + el_ref[at, :][None] * edge_left)
        )
        img_ref[:, at, :] = image
        return image

    def flat(value):
        return value.reshape(wide, cols)

    def gram_step(left, rights):
        lh, ll = split(left)
        highs, lows = zip(*[split(right) for right in rights])
        rh = jnp.concatenate(highs, axis=0) if len(highs) > 1 else highs[0]
        rl = jnp.concatenate(lows, axis=0) if len(lows) > 1 else lows[0]
        return fast_dot(
            jnp.concatenate([lh, lh, ll], axis=1), jnp.concatenate([rh, rl, rh], axis=1), ((1,), (1,))
        )

    def begin(r, carry):
        at = rows_at(r)
        store_direction(0, r, flat(b_ref[:, at, :] * inv_ref[at, :][None]))
        return carry

    for stage in range(ITERS):
        for side in range(2):
            vcol_src[stage, side] = jnp.zeros((wide, LANES), F32)
    lax.fori_loop(0, tiles, begin, 0)
    direction_start(0)

    g0_ref[...] = jnp.zeros((wide, wide), F32)

    def first_gram(p, carry):
        lefts = [flat(b_ref[:, rows_at(2 * p + h), :]) for h in range(2)]
        rights = [flat(v_ref[:, rows_at(2 * p + h + 1), :]) for h in range(2)]
        g0_ref[...] += gram_step(jnp.concatenate(lefts, axis=1), [jnp.concatenate(rights, axis=1)])
        return carry

    lax.fori_loop(0, pairs, first_gram, 0)

    pick = (iota((fields, wide), 1) // SUB == iota((fields, wide), 0)).astype(F32)
    same = lax.rem(iota((wide, wide), 0), SUB) == lax.rem(iota((wide, wide), 1), SUB)

    def reduced(block):
        part = exact_dot(pick, jnp.where(same, block, 0.0), ((1,), (0,)))
        return exact_dot(part, pick, ((1,), (1,)))

    def all_sum(stage, value):
        for phase, (count, me, slots, mine) in enumerate(
            ((nr, row, row_slots, row_mine), (nc, col, col_slots, col_mine))
        ):
            mine[stage] = value
            slots[stage, me] = value
            copies = []
            for d in range(1, count):
                peer = lax.rem(me + d, count)
                copies.append(
                    pltpu.make_async_remote_copy(
                        src_ref=mine.at[stage],
                        dst_ref=slots.at[stage, me],
                        send_sem=red_send.at[stage, phase, d],
                        recv_sem=red_recv.at[stage, phase, d],
                        device_id=(peer, col) if phase == 0 else (row, peer),
                        device_id_type=MESH,
                    )
                )
            for copy in copies:
                copy.start()
            for copy in copies:
                copy.wait()
            value = slots[stage, 0]
            for d in range(1, count):
                value = value + slots[stage, d]
        return value

    def kron(matrix):
        half = exact_dot(matrix, pick, ((0,), (0,)))
        full = exact_dot(pick, half, ((0,), (0,)))
        high, low = split(jnp.where(same, full, 0.0))
        return jnp.concatenate([high, high], axis=1), jnp.concatenate([low, low], axis=1)

    def combined(coefs, value):
        high, low = split(value)
        both = jnp.concatenate([high, low], axis=0)
        return [
            fast_dot(h, both, ((1,), (0,))) + fast_dot(l, both, ((1,), (0,))) for h, l in coefs
        ]

    rowf = iota((fields, LANES), 0)

    def padded(parts):
        spare = jnp.zeros((fields, LANES - fields * len(parts)), F32)
        return jnp.concatenate(list(parts) + [spare], axis=1)

    gram_now = None
    for step in range(ITERS):
        last = step == ITERS - 1
        direction_wait(step)
        terms = 1 if last else (2 if step == 0 else 3)
        span = terms * wide
        gram_ref[:, 0:span] = jnp.zeros((wide, span), F32)

        def stencil(p, carry, step=step, terms=terms, span=span):
            images, groups = [], [[] for _ in range(terms)]
            for h in range(2):
                r = 2 * p + h
                at = rows_at(r)
                image = operate(step, r)
                images.append(flat(image))
                groups[0].append(flat(v_ref[:, rows_at(r + 1), :]))
                if terms > 1:
                    groups[1].append(flat(image * inv_ref[at, :][None]))
                if terms > 2:
                    groups[2].append(flat(res_ref[:, at, :] * inv_ref[at, :][None]))
            gram_ref[:, 0:span] += gram_step(
                jnp.concatenate(images, axis=1), [jnp.concatenate(g, axis=1) for g in groups]
            )
            return carry

        lax.fori_loop(0, pairs, stencil, 0)
        parts = [reduced(gram_ref[:, t * wide:(t + 1) * wide]) for t in range(terms)]
        if step == 0:
            parts.append(reduced(g0_ref[...]))
        total = all_sum(step, padded(parts))
        curvature = total[:, 0:fields]
        if step == 0:
            gram_now = total[:, 2 * fields:3 * fields]
        system = padded([curvature, gram_now])
        unit = (iota((fields, fields), 0) == iota((fields, fields), 1)).astype(F32)
        other = padded([gram_now, unit])
        for j in range(fields):
            scaled = system[j:j + 1, :] / system[j:j + 1, j:j + 1]
            system = jnp.where(rowf == j, scaled, system - system[:, j:j + 1] * scaled)
            if not last:
                scaled = other[j:j + 1, :] / other[j:j + 1, j:j + 1]
                other = jnp.where(rowf == j, scaled, other - other[:, j:j + 1] * scaled)
        alpha = system[:, fields:2 * fields]
        coefs = [kron(alpha)]
        if not last:
            image_term = total[:, fields:2 * fields]
            cross = curvature if step == 0 else total[:, 2 * fields:3 * fields]
            mixed = exact_dot(alpha, cross, ((0,), (0,)))
            mixed_t = exact_dot(cross, alpha, ((0,), (0,)))
            quadratic = exact_dot(
                exact_dot(alpha, image_term, ((0,), (0,))), alpha, ((1,), (0,))
            )
            gram_next = gram_now - mixed - mixed_t + quadratic
            beta = exact_dot(other[:, fields:2 * fields], gram_next, ((1,), (0,)))
            coefs.append(kron(beta))
            gram_now = gram_next

        def update(p, carry, step=step, last=last, coefs=coefs):
            v = jnp.concatenate([flat(v_ref[:, rows_at(2 * p + h + 1), :]) for h in range(2)], axis=1)
            image = jnp.concatenate([flat(img_ref[:, rows_at(2 * p + h), :]) for h in range(2)], axis=1)
            moved = combined(coefs, v)
            drop = combined(coefs[:1], image)[0]
            for h in range(2):
                r = 2 * p + h
                at = rows_at(r)
                part = slice(h * cols, (h + 1) * cols)
                shift = moved[0][:, part].reshape(fields, SUB, cols)
                if step == 0:
                    sol_ref[:, at, :] = shift
                    old = b_ref[:, at, :]
                else:
                    sol_ref[:, at, :] += shift
                    old = res_ref[:, at, :]
                residual = old - drop[:, part].reshape(fields, SUB, cols)
                res_ref[:, at, :] = residual
                if not last:
                    store_direction(
                        step + 1, r, flat(residual * inv_ref[at, :][None]) + moved[1][:, part]
                    )
            return carry

        lax.fori_loop(0, pairs, update, 0)
        if not last:
            direction_start(step + 1)


def shards(right_side, cond_x, cond_y, pad_mask):
    fields, rows, cols = right_side.shape
    nr = lax.axis_size("row")
    nc = lax.axis_size("col")
    wide = fields * SUB
    vmem = lambda *shape: pltpu.VMEM(shape, F32)
    plane = vmem(rows, cols)
    out = jax.ShapeDtypeStruct(right_side.shape, F32)
    return pl.pallas_call(
        functools.partial(kernel, nr, nc),
        out_shape=(out, out),
        in_specs=[pl.BlockSpec(memory_space=pltpu.VMEM)] * 4,
        out_specs=(pl.BlockSpec(memory_space=pltpu.VMEM),) * 2,
        scratch_shapes=[
            vmem(fields, rows + 2 * SUB, cols),
            vmem(fields, rows, cols),
            plane, plane, plane, plane, plane, plane,
            vmem(wide, 3 * wide), vmem(wide, wide),
            vmem(2, SUB, cols), vmem(2, SUB, cols),
            vmem(2, 2 * SUB, LANES), vmem(2, 2 * SUB, LANES),
            vmem(ITERS, 2, fields, cols), vmem(ITERS, 2, fields, cols),
            vmem(ITERS, 2, wide, LANES), vmem(ITERS, 2, wide, LANES),
            vmem(ITERS, nr, fields, LANES), vmem(ITERS, nc, fields, LANES),
            vmem(ITERS, fields, LANES), vmem(ITERS, fields, LANES),
            pltpu.SemaphoreType.DMA((ITERS + 1, 4)), pltpu.SemaphoreType.DMA((ITERS + 1, 4)),
            pltpu.SemaphoreType.DMA((ITERS, 2, max(nr, nc))),
            pltpu.SemaphoreType.DMA((ITERS, 2, max(nr, nc))),
        ],
        compiler_params=pltpu.CompilerParams(
            collective_id=0, has_side_effects=True, vmem_limit_bytes=60 * 1024 * 1024
        ),
        name="block_cg",
    )(right_side, cond_x, cond_y, pad_mask)


def solution(mesh):
    in_specs = (P(None, "row", "col"), P("row", "col"), P("row", "col"), P("row", "col"))
    out_specs = (P(None, "row", "col"), P(None, "row", "col"))
    return jax.shard_map(shards, mesh=mesh, in_specs=in_specs, out_specs=out_specs, check_vma=False)
```

time: 516 us -> 140 us (0.27); the launches traced: 509 us -> 140 us
  matrix products: 186 us -> 0 us
  blocking collectives: 131 us -> 0 us
  Pallas kernels: 0 us -> 130 us
  other arithmetic: 101 us -> 0 us
  local copies, waits for them, and re-layouts: 45.3 us -> 8.95 us
  starting transfers between devices: 30 us -> 0 us
  waiting for transfers between devices: 15 us -> 0 us
    dot_general x22 -> x0, matrix products: 184 us -> none  [the longest x8 95.2 us: gram(): return jnp.einsum('kab,lab->kl', left, right, precision=exact_precision)]
    psum x3 -> x0, blocking collectives: 131 us -> none  [the longest x2 84.9 us: shards(): lax.psum((gram(direction, image), gram(image, precond), gram(image, weigh...]
    pallas_call x0 -> x1, Pallas kernels: none -> 130 us  [shards(): pl.pallas_call(functools.partial(kernel, nr, nc), out_shape=(out, out), i...]
    add x4 -> x0, other arithmetic: 63.9 us -> none  [the longest x3 61.2 us: shards(): pad_nodes * direction]
    ppermute x14 -> x0, starting transfers between devices: 30 us -> none  [the longest x6 15.2 us: extended(): lax.ppermute(tail, axis, [(i, (i + 1) % count) for i in range(ends)])]
    another operation x25 -> x0, other arithmetic: 20.1 us -> none  [the longest x15 10.8 us: small_solve(): factor = jnp.linalg.cholesky(matrix)]
    slice x11 -> x0, local copies, waits for them, and re-layouts: 17.4 us -> none  [the longest x6 7.86 us: extended(): lax.slice_in_dim(cells, cells.shape[dim] - width, cells.shape[dim], axis=...]
    ppermute x6 -> x0, local copies, waits for them, and re-layouts: 15.3 us -> none  [the longest x3 7.7 us: extended(): lax.ppermute(head, axis, [((i + 1) % count, i) for i in range(ends)])]
  transfers between devices with their start and end apart: 14 -> 0, of which waited for: 5 -> 0; matrix products, arithmetic and copies ran while one was open for 10% -> 0% of each run, Pallas kernels for 0% -> 0%
where the time goes in v1:
time: 140 us
  Pallas kernels  130 us (93%)
  local copies, waits for them, and re-layouts  8.95 us (6%)
    pallas_call x1, Pallas kernels, shards(): pl.pallas_call(functools.partial(kernel, nr, nc), out_shape=(out, out), i...  130 us
    unnamed x4, local copies, waits for them, and re-layouts  8.95 us

profile of v1, /device:TPU:0, one launch (start us, length us, event | category | flops | bytes accessed | tf_op | source)
XLA Modules:
  0.0 139.7 jit_solution(17234774583169223222)
XLA Ops:
  0.6 130.1 %block_cg.1 = (f32[16,256,384]{2,1,0:T(8,128)}, f32[16,256,384]{2,1,0:T(8,128)}) custom-call(f32[16,256,384]{2,1,0:T(8,128)} %b_ref.1, f32[256,384]{1,0:T(8,128)} %cx_ref.1, f32[256,384]{1,0:T(8,128)} %cy_ref.1, s32[256,384]{1,0:T(8,128)} %pad_ref.1), custom_call_target="tpu_custom_call" | custom-call | tf_op jit(solution)/shard_map/block_cg/pallas_call | solution.py:397
  130.7 0.0 copy-start
  130.7 6.2 %copy.8 = f32[16,256,384]{2,1,0:T(8,128)} copy(f32[16,256,384]{2,1,0:T(8,128)} %get-tuple-element.4) | data formatting | bytes 12582912
  137.0 0.0 copy-done
  137.0 2.7 %copy.9 = f32[16,256,384]{2,1,0:T(8,128)} copy(f32[16,256,384]{2,1,0:T(8,128)S(1)} %copy-done) | data formatting | bytes 12582912
Async XLA Ops:
  130.7 6.3 %copy-start = (f32[16,256,384]{2,1,0:T(8,128)S(1)}, f32[16,256,384]{2,1,0:T(8,128)}, u32[]{:S(2)}) copy-start(f32[16,256,384]{2,1,0:T(8,128)} %get-tuple-element.5) | copy-start | bytes 18874372
